TPU v7x, 32 devices: a whole 2x2x4 slice. The times are simulated.
32 devices in a mesh: seq: 2 (over x), tensor: 4 (over z), bucket: 4 (over y, core).
Axes of the slice: x: 2, y: 2, z: 4, core: 2. Of those that a mesh axis runs over, the one named last changes fastest.
Arguments:
- queries: bfloat16 [4, 1024, 3072], P('bucket', ('seq', 'tensor')), may hold values from -6 to 6
- keys: bfloat16 [4, 1024, 3072], P('bucket', ('seq', 'tensor')), may hold values from -6 to 6
- values: bfloat16 [4, 1024, 3072], P('bucket', ('seq', 'tensor')), may hold values from -6 to 6
- lengths: int32 [4], P('bucket'), may hold values from 256 to 1024, as said below
- out_weight: bfloat16 [3072, 3072], P(('seq', 'bucket'), 'tensor'), may hold values from -0.109375 to 0.109375
Outputs:
- projected: bfloat16 [4, 1024, 3072], P('bucket', ('seq', 'tensor'))
Inputs may be any that keep to these rules, and one draw needn't show every extreme that they name: `lengths`: each bucket has 256 to 1024 live tokens, and at least one bucket has all 1024.
All inputs are finite; a program needn't handle non-finite values.
Results may differ from a plain program's by a relative error of at most 0.018.
Values may be sent and summed in bfloat16 or wider, within the bound.
A program may use at most 128 MiB of HBM per device.

v0:
```python
import jax
import jax.numpy as jnp
from jax import lax
from jax.sharding import PartitionSpec as P

HS = 128


MASKED_SCORE = -1e30


def shards(queries, keys, values, lengths, out_weight):
    tok_rows = queries.shape[1]
    n_tensor = lax.axis_size("tensor")
    tensor_index = lax.axis_index("tensor")
    live_len = lengths[0]
    local_q, local_k, local_v = (
        lax.all_to_all(queries[0], "seq", split_axis=1, concat_axis=0, tiled=True),
        lax.all_to_all(keys[0], "seq", split_axis=1, concat_axis=0, tiled=True),
        lax.all_to_all(values[0], "seq", split_axis=1, concat_axis=0, tiled=True),
    )
    row_count, col_count = local_q.shape
    head_count = col_count // HS
    query_heads = local_q.reshape(row_count, head_count, HS)

    def spots(first_row, total_rows):
        index_row = first_row + jnp.arange(total_rows, dtype=jnp.int32)
        owner = index_row // row_count
        within = index_row % row_count
        return (within // tok_rows * n_tensor + owner) * tok_rows + within % tok_rows

    query_usable = spots(tensor_index * row_count, row_count) < live_len
    initial = (
        jnp.full((row_count, head_count), MASKED_SCORE, jnp.float32),
        jnp.zeros((row_count, head_count), jnp.float32),
        jnp.zeros((row_count, head_count, HS), jnp.float32),
    )
    carried = initial
    first_row = jnp.int32(0)
    key_rows = lax.all_gather(local_k, "tensor", axis=0, tiled=True)
    value_rows = lax.all_gather(local_v, "tensor", axis=0, tiled=True)
    for offset in range(key_rows.shape[0] // row_count):
        row_peak, row_sum, accumulated = carried
        key_tile = key_rows[offset * row_count : (offset + 1) * row_count].reshape(
            row_count, head_count, HS
        )
        value_tile = value_rows[offset * row_count : (offset + 1) * row_count].reshape(
            row_count, head_count, HS
        )
        key_usable = spots(first_row + offset * row_count, row_count) < live_len
        scores = jnp.einsum(
            "qhd,khd->qhk", query_heads, key_tile, preferred_element_type=jnp.float32
        ) * HS ** (-0.5)
        scores = jnp.where(key_usable[None, None, :], scores, MASKED_SCORE)
        peak_new = jnp.maximum(row_peak, jnp.max(scores, axis=-1))
        exponent = jnp.where(key_usable[None, None, :], jnp.exp(scores - peak_new[..., None]), 0.0)
        rescale = jnp.exp(row_peak - peak_new)
        accumulated = accumulated * rescale[..., None] + jnp.einsum(
            "qhk,khd->qhd",
            exponent.astype(jnp.bfloat16),
            value_tile,
            preferred_element_type=jnp.float32,
        )
        carried = (peak_new, row_sum * rescale + jnp.sum(exponent, axis=-1), accumulated)
    row_peak, row_sum, accumulated = carried
    attended = accumulated / row_sum[..., None]
    mixed = jnp.where(query_usable[:, None], attended.reshape(row_count, col_count), 0.0).astype(
        jnp.bfloat16
    )
    restored = lax.all_to_all(mixed, "seq", split_axis=0, concat_axis=1, tiled=True)
    wide_weight = lax.all_gather(out_weight, "tensor", axis=1, tiled=True)
    summed = jnp.dot(
        restored,
        lax.all_gather(wide_weight, ("seq", "bucket"), axis=0, tiled=True),
        preferred_element_type=jnp.float32,
    )
    return summed.astype(jnp.bfloat16)[None]


def solution(mesh):
    in_specs = (
        P("bucket", ("seq", "tensor"), None),
        P("bucket", ("seq", "tensor"), None),
        P("bucket", ("seq", "tensor"), None),
        P("bucket"),
        P(("seq", "bucket"), "tensor"),
    )
    out_specs = P("bucket", ("seq", "tensor"), None)
    return jax.shard_map(shards, mesh=mesh, in_specs=in_specs, out_specs=out_specs, check_vma=False)
```

profile of v0, /device:TPU:0, one launch (start us, length us, event | category | flops | bytes accessed | tf_op | source)
XLA Modules:
  0.0 309.9 jit_solution(5005568359367810147)
XLA Ops:
  7.3 1.5 copy.68
  8.8 14.8 %all_to_all.70 = bf16[128,2,1536]{0,2,1:T(8,128)(2,1)S(1)} all-to-all(bf16[128,2,1536]{0,2,1:T(8,128)(2,1)S(1)} %bitcast.125), channel_id=1, replica_groups=mesh['seq'=2,'tensor'=4,'bucket'=4] {'seq'}, dimensions={1} | all-to-all | bytes 1572864 | tf_op jit(solution)/shard_map/all_to_all | solution.py:19
  23.6 1.2 copy.69
  25.3 12.5 %all_to_all.71 = bf16[128,2,1536]{0,2,1:T(8,128)(2,1)S(1)} all-to-all(bf16[128,2,1536]{0,2,1:T(8,128)(2,1)S(1)} %bitcast.126), channel_id=1, replica_groups=mesh['seq'=2,'tensor'=4,'bucket'=4] {'seq'}, dimensions={1} | all-to-all | bytes 1572864 | tf_op jit(solution)/shard_map/all_to_all | solution.py:20
  37.8 1.2 copy.76
  39.0 22.6 %all-gather.9.cloned.1.call-done = bf16[384,3072]{1,0:T(8,128)(2,1)} async-done(((bf16[384,768]{1,0:T(8,128)(2,1)}), bf16[384,3072]{1,0:T(8,128)(2,1)}) %all-gather.9.cloned.1.call-update) | async-done | bytes 2359312 | tf_op jit(solution)/shard_map/all_gather | solution.py:71
  61.7 1.2 copy.71
  62.8 3.5 %all-to-all-start.1 = ((bf16[128,2,1536]{0,2,1:T(8,128)(2,1)}), bf16[128,2,1536]{0,2,1:T(8,128)(2,1)S(1)}, u32[]{:S(2)}, u32[]{:S(2)}) async-start(bf16[128,2,1536]{0,2,1:T(8,128)(2,1)} %bitcast.5), calls=%async_computation.1 | async-start | bytes 1572864 | tf_op jit(solution)/shard_map/all_to_all | solution.py:18
  67.1 10.2 %all-to-all-done.1 = bf16[128,2,1536]{0,2,1:T(8,128)(2,1)S(1)} async-done(((bf16[128,2,1536]{0,2,1:T(8,128)(2,1)}), bf16[128,2,1536]{0,2,1:T(8,128)(2,1)S(1)}, u32[]{:S(2)}, u32[]{:S(2)}) %all-to-all-start.1) | async-done | bytes 786464 | tf_op jit(solution)/shard_map/all_to_all | solution.py:18
  77.3 6.7 %copy.72 = bf16[2,128,1536]{1,0,2:T(2,128)(2,1)S(1)} copy(bf16[2,128,1536]{1,2,0:T(8,128)(2,1)S(1)} %bitcast.122) | data formatting | bytes 1572864 | tf_op jit(solution)/shard_map/all_to_all | solution.py:18
  84.4 41.0 %all-gather.5.cloned.1.call-done = bf16[1024,1536]{1,0:T(8,128)(2,1)} async-done(((bf16[256,1536]{1,0:T(8,128)(2,1)}), bf16[1024,1536]{1,0:T(8,128)(2,1)}) %all-gather.5.cloned.1.call-update) | async-done | bytes 3145744 | tf_op jit(solution)/shard_map/all_gather | solution.py:40
  125.4 2.9 fusion.89
  128.4 1.2 copy.70
  130.1 1.4 copy.80
  131.5 57.6 %all-gather.7.cloned.1.call-done = bf16[1024,1536]{1,0:T(8,128)(2,1)} async-done(((bf16[256,1536]{1,0:T(8,128)(2,1)}), bf16[1024,1536]{1,0:T(8,128)(2,1)}) %all-gather.7.cloned.1.call-update) | async-done | bytes 3145744 | tf_op jit(solution)/shard_map/all_gather | solution.py:41
  189.1 3.6 %fusion.88 = (bf16[256,1536]{1,0:T(8,128)(2,1)}, bf16[256,1536]{1,0:T(8,128)(2,1)}, bf16[256,1536]{1,0:T(8,128)(2,1)}, bf16[256,1536]{1,0:T(8,128)(2,1)}) fusion(bf16[1024,1536]{1,0:T(8,128)(2,1)} %all-gather.7.cloned.1.call-done), kind=kLoop, calls=%fused_computation.155 | loop fusion | bytes 6291456 | tf_op jit(solution)/shard_map/slice | solution.py:47
  192.7 2.3 copy.83
  195.0 2.5 copy.89
  197.5 2.4 copy.95
  199.9 2.5 copy.77
  202.4 1.9 bitcast_reduce_fusion.3
  204.3 0.8 bitcast_reduce_fusion
  205.2 0.8 bitcast_reduce_fusion.1
  206.1 0.8 bitcast_reduce_fusion.2
  208.6 0.8 fusion.15
  210.4 1.2 fusion.21
  211.6 1.4 fusion.19
  212.9 1.2 fusion.17
  214.2 3.0 fusion.25
  218.6 16.7 %all_to_all.72 = bf16[2,128,1536]{1,2,0:T(8,128)(2,1)S(1)} all-to-all(bf16[2,128,1536]{1,2,0:T(8,128)(2,1)S(1)} %copy.99), channel_id=1, replica_groups=mesh['seq'=2,'tensor'=4,'bucket'=4] {'seq'}, dimensions={0} | all-to-all | bytes 1572864 | tf_op jit(solution)/shard_map/all_to_all | solution.py:70
  235.3 58.3 %all-gather.11.cloned.1.call-done = bf16[3072,3072]{1,0:T(8,128)(2,1)} async-done(((bf16[384,3072]{1,0:T(8,128)(2,1)}), bf16[3072,3072]{1,0:T(8,128)(2,1)}) %all-gather.11.cloned.1.call-update) | async-done | bytes 18874384 | tf_op jit(solution)/shard_map/all_gather | solution.py:74
  293.5 9.9 %fusion = bf16[1,128,3072]{2,1,0:T(8,128)(2,1)} fusion(bf16[128,3072]{0,1:T(8,128)(2,1)S(1)} %bitcast.115, bf16[3072,3072]{1,0:T(8,128)(2,1)} %all-gather.11.cloned.1.call-done), kind=kOutput, calls=%fused_computation.1 | convolution fusion | flops 2416312320 | bytes 20447232 | tf_op jit(solution)/shard_map/dot_general | solution.py:72
  (36 shorter events, 6.3 us)
Async XLA Ops:
  6.5 18.3 %copy-start = (bf16[1,128,3072]{2,1,0:T(8,128)(2,1)S(1)}, bf16[1,128,3072]{2,1,0:T(8,128)(2,1)}, u32[]{:S(2)}) copy-start(bf16[1,128,3072]{2,1,0:T(8,128)(2,1)} %param.7) | copy-start | bytes 2359300
  6.5 55.1 %all-gather.9.cloned.1.call-start = ((), (), s32[]{:S(2)}) async-start(), calls=%async_computation.6 | async-start | bytes 2949120 | tf_op jit(solution)/shard_map/all_gather | solution.py:71
  7.3 118.2 %all-gather.5.cloned.1.call-start = ((), (), s32[]{:S(2)}) async-start(), calls=%async_computation.4 | async-start | bytes 3932160 | tf_op jit(solution)/shard_map/all_gather | solution.py:40
  24.8 164.3 %all-gather.7.cloned.1.call-start = ((), (), s32[]{:S(2)}) async-start(), calls=%async_computation.5 | async-start | bytes 3932160 | tf_op jit(solution)/shard_map/all_gather | solution.py:41
  25.3 36.4 %copy-start.1 = (bf16[1,128,3072]{2,1,0:T(8,128)(2,1)S(1)}, bf16[1,128,3072]{2,1,0:T(8,128)(2,1)}, u32[]{:S(2)}) copy-start(bf16[1,128,3072]{2,1,0:T(8,128)(2,1)} %param.5) | copy-start | bytes 2359300
  39.0 254.6 %all-gather.11.cloned.1.call-start = ((), (), s32[]{:S(2)}) async-start(), calls=%async_computation.7 | async-start | bytes 21233664 | tf_op jit(solution)/shard_map/all_gather | solution.py:74
  62.8 14.4 %all-to-all-start.1 = ((bf16[128,2,1536]{0,2,1:T(8,128)(2,1)}), bf16[128,2,1536]{0,2,1:T(8,128)(2,1)S(1)}, u32[]{:S(2)}, u32[]{:S(2)}) async-start(bf16[128,2,1536]{0,2,1:T(8,128)(2,1)} %bitcast.5), calls=%async_computation.1 | async-start | bytes 1572864 | tf_op jit(solution)/shard_map/all_to_all | solution.py:18
  208.6 1.7 copy-start.5
  210.4 1.2 copy-start.4
  211.6 1.4 copy-start.3
  212.9 1.2 copy-start.2
Sparse Core Ops, SparseCore 0:
  8.9 52.6 all-gather.8
  63.2 62.1 all-gather.4
  127.0 62.0 all-gather.6
  190.9 102.6 all-gather.10
where the time goes:
time: 311 us; the launch traced here: 310 us
  waiting for transfers between devices  190 us (61%)
  blocking collectives  44 us (14%)
  local copies, waits for them, and re-layouts  32.5 us (10%)
  matrix products  21.1 us (7%)
  between operations  14.1 us (5%)
  other arithmetic  4.22 us (1%)
  starting transfers between devices  3.66 us (1%)
    all_gather x1, waiting for transfers between devices, shards(): lax.all_gather(wide_weight, ('seq', 'bucket'), axis=0, tiled=True)  58.3 us
    all_gather x1, waiting for transfers between devices, shards(): value_rows = lax.all_gather(local_v, 'tensor', axis=0, tiled=True)  57.6 us
    all_gather x1, waiting for transfers between devices, shards(): key_rows = lax.all_gather(local_k, 'tensor', axis=0, tiled=True)  41 us
    all_gather x1, waiting for transfers between devices, shards(): wide_weight = lax.all_gather(out_weight, 'tensor', axis=1, tiled=True)  22.6 us
    all_to_all x1, blocking collectives, shards(): lax.all_to_all(mixed, 'seq', split_axis=0, concat_axis=1, tiled=True)  16.7 us
    all_to_all x1, blocking collectives, shards(): lax.all_to_all(keys[0], 'seq', split_axis=1, concat_axis=0, tiled=True)  14.8 us
    slice x5, local copies, waits for them, and re-layouts, shards(): value_rows[offset * row_count:(offset + 1) * row_count]  13.3 us
    all_to_all x1, blocking collectives, shards(): lax.all_to_all(values[0], 'seq', split_axis=1, concat_axis=0, tiled=True)  12.5 us
  transfers between devices with their start and end apart: 5, of which 5 were waited for; matrix products, arithmetic and copies ran while one was open for 15% of the time, Pallas kernels for 0%

commit v1 on v0

--- a/solution.py
+++ b/solution.py
@@ -1,6 +1,11 @@
+import functools
+import math
+
 import jax
 import jax.numpy as jnp
 from jax import lax
+from jax.experimental import pallas as pl
+from jax.experimental.pallas import tpu as pltpu
 from jax.sharding import PartitionSpec as P
 
 HS = 128
@@ -77,6 +82,277 @@
     return summed.astype(jnp.bfloat16)[None]
 
 
+def whole_kernel(
+    axes, sizes, len_ref, q_ref, k_ref, v_ref, w_ref, out_ref,
+    got, done, mixed, weight, part_out, part_in, own_part,
+    qkv_send, qkv_recv, att_send, att_recv, up_send, down_send, line_recv,
+    far_send, far_recv, near_send, near_recv, part_send, part_recv,
+):
+    n_seq, n_tensor, n_bucket = sizes
+    s, t, b = lax.axis_index("seq"), lax.axis_index("tensor"), lax.axis_index("bucket")
+    group = n_seq * n_tensor
+    rows = q_ref.shape[1]
+    width = q_ref.shape[2]
+    heads = width // HS // group
+    w_rows, w_cols = w_ref.shape
+    block = n_seq * rows
+    live = len_ref[0]
+
+    def device(ds, dt, db):
+        place = {"seq": ds, "tensor": dt, "bucket": db}
+        return tuple(place[name] for name in axes)
+
+    def remote(src, dst, send, recv, where):
+        return pltpu.make_async_remote_copy(
+            src_ref=src, dst_ref=dst, send_sem=send, recv_sem=recv,
+            device_id=where, device_id_type=pl.DeviceIdType.MESH,
+        )
+
+    me = s * n_tensor + t
+    streams = (q_ref, k_ref, v_ref)
+
+    def spot(ds, dt):
+        return pl.ds(pl.multiple_of((dt * n_seq + ds) * rows, rows), rows)
+
+    def qkv_copy(h, j, step, peer, source):
+        cols = pl.ds(pl.multiple_of((peer * heads + h) * HS, HS), HS)
+        return remote(
+            streams[j].at[0, :, cols],
+            got.at[h, j, spot(source // n_tensor, source % n_tensor), :],
+            qkv_send.at[h, j, step],
+            qkv_recv.at[h, j, step],
+            device(peer // n_tensor, peer % n_tensor, b),
+        )
+
+    def start_qkv(h):
+        def body(step, carry):
+            peer = (me + step) % group
+            for j in range(3):
+                qkv_copy(h, j, step, peer, me).start()
+            return carry
+
+        lax.fori_loop(1, group, body, 0)
+
+    def piece(row_block, col_block):
+        return weight.at[
+            pl.ds(pl.multiple_of(row_block * w_rows, w_rows), w_rows),
+            pl.ds(pl.multiple_of(col_block * w_cols, w_cols), w_cols),
+        ]
+
+    far, near = (b + 2) % 4, b + 1 - 2 * (b % 2)
+
+    def up_copy(p):
+        return remote(piece(b, p), piece(b, p), up_send.at[p], line_recv.at[p], device(s, t + 1, b))
+
+    def down_copy(p):
+        return remote(piece(b, p), piece(b, p), down_send.at[p], line_recv.at[p], device(s, t - 1, b))
+
+    def far_copy(p, row_block):
+        return remote(piece(row_block, p), piece(row_block, p), far_send.at[p], far_recv.at[p], device(s, t, far))
+
+    def near_copy(k, p, row_block):
+        return remote(
+            piece(row_block, p), piece(row_block, p), near_send.at[k, p], near_recv.at[k, p], device(s, t, near)
+        )
+
+    def spread(p):
+        far_copy(p, b).start()
+        near_copy(0, p, b).start()
+
+    def relay(k):
+        @pl.when(t >= k)
+        def _():
+            up_copy(t - k).wait_recv()
+
+            @pl.when(t < n_tensor - 1)
+            def _():
+                up_copy(t - k).start()
+
+            spread(t - k)
+
+        @pl.when(t + k < n_tensor)
+        def _():
+            down_copy(t + k).wait_recv()
+
+            @pl.when(t > 0)
+            def _():
+                down_copy(t + k).start()
+
+            spread(t + k)
+
+    start_qkv(0)
+    weight[
+        pl.ds(pl.multiple_of(b * w_rows, w_rows), w_rows),
+        pl.ds(pl.multiple_of(t * w_cols, w_cols), w_cols),
+    ] = w_ref[...]
+    spread(t)
+    for h in range(1, heads):
+        start_qkv(h)
+
+    @pl.when(t < n_tensor - 1)
+    def _():
+        up_copy(t).start()
+
+    @pl.when(t > 0)
+    def _():
+        down_copy(t).start()
+
+    for h in range(heads):
+        cols = pl.ds(pl.multiple_of((me * heads + h) * HS, HS), HS)
+        for j in range(3):
+            got[h, j, spot(s, t), :] = streams[j][0, :, cols]
+
+    total = group * rows
+    index = lax.broadcasted_iota(jnp.int32, (1, total), 1)
+    token = (index % block // rows * n_tensor + index // block) * rows + index % rows
+    usable = token < live
+    row_index = lax.broadcasted_iota(jnp.int32, (block, 1), 0)
+    factor = HS ** (-0.5) * math.log2(math.e)
+
+    def att_copy(h, step, target, source):
+        here = pl.ds(pl.multiple_of(target * block, block), block)
+        cols = pl.ds(pl.multiple_of((source * heads + h) * HS, HS), HS)
+        return remote(
+            done.at[h, here, :], mixed.at[:, cols], att_send.at[h, step], att_recv.at[h, step], device(s, target, b)
+        )
+
+    def attend(h, target):
+        here = pl.ds(pl.multiple_of(target * block, block), block)
+        scores = lax.dot_general(
+            got[h, 0, here, :], got[h, 1], (((1,), (1,)), ((), ())), preferred_element_type=jnp.float32
+        )
+        scores = jnp.where(usable, scores, MASKED_SCORE)
+        peak = jnp.max(scores, axis=-1, keepdims=True)
+        expo = jnp.exp2((scores - peak) * factor)
+        denominator = jnp.sum(expo, axis=-1, keepdims=True)
+        result = jnp.dot(expo.astype(jnp.bfloat16), got[h, 2], preferred_element_type=jnp.float32) / denominator
+        own_token = (row_index // rows * n_tensor + target) * rows + row_index % rows
+        return jnp.where(own_token < live, result, 0.0).astype(jnp.bfloat16)
+
+    for h in range(heads):
+        def arrive(step, carry):
+            source = (me + group - step) % group
+            for j in range(3):
+                qkv_copy(h, j, step, me, source).wait_recv()
+            return carry
+
+        lax.fori_loop(1, group, arrive, 0)
+
+        def one(step, carry):
+            target = (t + step) % n_tensor
+            here = pl.ds(pl.multiple_of(target * block, block), block)
+            done[h, here, :] = attend(h, target)
+            att_copy(h, step, target, t).start()
+            return carry
+
+        lax.fori_loop(1, n_tensor, one, 0)
+        mixed[:, pl.ds(pl.multiple_of((t * heads + h) * HS, HS), HS)] = attend(h, t)
+        if h + 1 < n_tensor:
+            relay(h + 1)
+    for k in range(heads + 1, n_tensor):
+        relay(k)
+
+    for p in range(n_tensor):
+        far_copy(p, far).wait_recv()
+        near_copy(1, p, far).start()
+    for p in range(n_tensor):
+        near_copy(0, p, near).wait_recv()
+        near_copy(1, p, (near + 2) % 4).wait_recv()
+    for h in range(heads):
+        def back(step, carry):
+            att_copy(h, step, t, (t + n_tensor - step) % n_tensor).wait_recv()
+            return carry
+
+        lax.fori_loop(1, n_tensor, back, 0)
+
+    def part_copy(p):
+        cut = slice(p * w_cols, (p + 1) * w_cols)
+        return remote(
+            part_out.at[:, cut], part_in.at[:, cut], part_send.at[p], part_recv.at[p], device(1 - s, t, b)
+        )
+
+    for p in range(n_tensor):
+        cut = slice(p * w_cols, (p + 1) * w_cols)
+        summed = jnp.dot(mixed[...], weight[:, cut], preferred_element_type=jnp.float32)
+        first, second = summed[:rows], summed[rows:]
+        part_out[:, cut] = jnp.where(s == 0, second, first).astype(jnp.bfloat16)
+        part_copy(p).start()
+        own_part[:, cut] = jnp.where(s == 0, first, second)
+    for p in range(n_tensor):
+        cut = slice(p * w_cols, (p + 1) * w_cols)
+        part_copy(p).wait_recv()
+        out_ref[0, :, cut] = (own_part[:, cut] + part_in[:, cut].astype(jnp.float32)).astype(jnp.bfloat16)
+
+    for h in range(heads):
+        def sent(step, carry):
+            peer = (me + step) % group
+            for j in range(3):
+                qkv_copy(h, j, step, peer, me).wait_send()
+            return carry
+
+        lax.fori_loop(1, group, sent, 0)
+
+        def att_sent(step, carry):
+            att_copy(h, step, (t + step) % n_tensor, t).wait_send()
+            return carry
+
+        lax.fori_loop(1, n_tensor, att_sent, 0)
+    for k in range(n_tensor):
+        @pl.when((t >= k) & (t < n_tensor - 1))
+        def _():
+            up_copy(t - k).wait_send()
+
+        @pl.when((t + k < n_tensor) & (t > 0))
+        def _():
+            down_copy(t + k).wait_send()
+
+    for p in range(n_tensor):
+        far_copy(p, b).wait_send()
+        near_copy(0, p, b).wait_send()
+        near_copy(1, p, far).wait_send()
+        part_copy(p).wait_send()
+
+
+def fused(axes, sizes, queries, keys, values, lengths, out_weight):
+    n_seq, n_tensor, n_bucket = sizes
+    rows, width = queries.shape[1:]
+    group = n_seq * n_tensor
+    heads = width // HS // group
+    total = group * rows
+    half = width // n_seq
+    vmem = pl.BlockSpec(memory_space=pltpu.VMEM)
+    dma = pltpu.SemaphoreType.DMA
+    return pl.pallas_call(
+        functools.partial(whole_kernel, axes, sizes),
+        out_shape=jax.ShapeDtypeStruct(queries.shape, queries.dtype),
+        in_specs=[pl.BlockSpec(memory_space=pltpu.SMEM), vmem, vmem, vmem, vmem],
+        out_specs=vmem,
+        scratch_shapes=[
+            pltpu.VMEM((heads, 3, total, HS), jnp.bfloat16),
+            pltpu.VMEM((heads, total, HS), jnp.bfloat16),
+            pltpu.VMEM((n_seq * rows, half), jnp.bfloat16),
+            pltpu.VMEM((half, width), jnp.bfloat16),
+            pltpu.VMEM((rows, width), jnp.bfloat16),
+            pltpu.VMEM((rows, width), jnp.bfloat16),
+            pltpu.VMEM((rows, width), jnp.float32),
+            dma((heads, 3, group)),
+            dma((heads, 3, group)),
+            dma((heads, n_tensor)),
+            dma((heads, n_tensor)),
+            dma((n_tensor,)),
+            dma((n_tensor,)),
+            dma((n_tensor,)),
+            dma((n_tensor,)),
+            dma((n_tensor,)),
+            dma((2, n_tensor)),
+            dma((2, n_tensor)),
+            dma((n_tensor,)),
+            dma((n_tensor,)),
+        ],
+        compiler_params=pltpu.CompilerParams(has_side_effects=True, vmem_limit_bytes=56 * 1024 * 1024),
+    )(lengths, queries, keys, values, out_weight)
+
+
 def solution(mesh):
     in_specs = (
         P("bucket", ("seq", "tensor"), None),
@@ -86,4 +362,13 @@
         P(("seq", "bucket"), "tensor"),
     )
     out_specs = P("bucket", ("seq", "tensor"), None)
-    return jax.shard_map(shards, mesh=mesh, in_specs=in_specs, out_specs=out_specs, check_vma=False)
+    sizes = tuple(mesh.shape[name] for name in ("seq", "tensor", "bucket"))
+
+    def step(queries, keys, values, lengths, out_weight):
+        head_count = queries.shape[2] // HS
+        fits = sizes[0] == 2 and sizes[1] == sizes[2] == 4 and head_count % (sizes[0] * sizes[1]) == 0
+        if fits:
+            return fused(mesh.axis_names, sizes, queries, keys, values, lengths, out_weight)
+        return shards(queries, keys, values, lengths, out_weight)
+
+    return jax.shard_map(step, mesh=mesh, in_specs=in_specs, out_specs=out_specs, check_vma=False)

time: 311 us -> 155 us (0.50)
  waiting for transfers between devices: 190 us -> 0 us
  Pallas kernels: 0 us -> 151 us
  blocking collectives: 44 us -> 0 us
  local copies, waits for them, and re-layouts: 32.5 us -> 2.06 us
  matrix products: 21.1 us -> 0 us
  between operations: 14.1 us -> 0.66 us
  other arithmetic: 4.22 us -> 0 us
  starting transfers between devices: 3.66 us -> 0 us
    all_gather x4 -> x0, waiting for transfers between devices: 180 us -> none  [the longest x1 58.3 us: shards(): lax.all_gather(wide_weight, ('seq', 'bucket'), axis=0, tiled=True)]
    pallas_call x0 -> x1, Pallas kernels: none -> 151 us  [fused(): pl.pallas_call(functools.partial(whole_kernel, axes, sizes), out_shape=ja...]
    all_to_all x3 -> x0, blocking collectives: 44 us -> none  [the longest x1 16.7 us: shards(): lax.all_to_all(mixed, 'seq', split_axis=0, concat_axis=1, tiled=True)]
    dot_general x9 -> x0, matrix products: 21.1 us -> none  [the longest x1 9.88 us: shards(): jnp.dot(restored, lax.all_gather(wide_weight, ('seq', 'bucket'), axis=0,...]
    slice x10 -> x0, local copies, waits for them, and re-layouts: 19.3 us -> none  [the longest x5 13.3 us: shards(): value_rows[offset * row_count:(offset + 1) * row_count]]
    all_to_all x1 -> x0, waiting for transfers between devices: 10.2 us -> none  [shards(): lax.all_to_all(queries[0], 'seq', split_axis=1, concat_axis=0, tiled=True)]
    all_to_all x3 -> x0, local copies, waits for them, and re-layouts: 9 us -> none  [the longest x1 6.67 us: shards(): lax.all_to_all(queries[0], 'seq', split_axis=1, concat_axis=0, tiled=True)]
    all_to_all x1 -> x0, starting transfers between devices: 3.53 us -> none  [shards(): lax.all_to_all(queries[0], 'seq', split_axis=1, concat_axis=0, tiled=True)]
  transfers between devices with their start and end apart: 5 -> 0, of which waited for: 5 -> 0; matrix products, arithmetic and copies ran while one was open for 15% -> 0% of each run, Pallas kernels for 0% -> 0%
where the time goes in v1:
time: 155 us; the launch traced here: 154 us
  Pallas kernels  151 us (97%)
  local copies, waits for them, and re-layouts  2.06 us (1%)
    pallas_call x1, Pallas kernels, fused(): pl.pallas_call(functools.partial(whole_kernel, axes, sizes), out_shape=ja...  151 us

profile of v1, /device:TPU:0, one launch (start us, length us, event | category | flops | bytes accessed | tf_op | source)
XLA Modules:
  0.0 154.1 jit_solution(5806552899946823329)
XLA Ops:
  0.7 151.4 %shard_map.55 = bf16[1,128,3072]{2,1,0:T(8,128)(2,1)} custom-call(s32[1]{0:T(128)S(6)} %copy.7.len_ref, bf16[1,128,3072]{2,1,0:T(8,128)(2,1)} %q_ref.1, bf16[1,128,3072]{2,1,0:T(8,128)(2,1)} %k_ref.1, bf16[1,128,3072]{2,1,0:T(8,128)(2,1)} %v_ref.1, bf16[384,768]{1,0:T(8,128)(2,1)} %w_ref.1), custom_call_target="tpu_custom_call" | custom-call | tf_op jit(solution)/shard_map/pallas_call | solution.py:325
  152.0 2.1 %copy.8 = bf16[1,128,3072]{2,1,0:T(8,128)(2,1)} copy(bf16[1,128,3072]{2,1,0:T(8,128)(2,1)} %shard_map.55) | data formatting | bytes 1572864

commit v2 on v1

--- a/solution.py
+++ b/solution.py
@@ -86,7 +86,7 @@
     axes, sizes, len_ref, q_ref, k_ref, v_ref, w_ref, out_ref,
     got, done, mixed, weight, part_out, part_in, own_part,
     qkv_send, qkv_recv, att_send, att_recv, up_send, down_send, line_recv,
-    far_send, far_recv, near_send, near_recv, part_send, part_recv,
+    far_send, far_recv, near_send, near_recv, part_send, part_recv, out_sem,
 ):
     n_seq, n_tensor, n_bucket = sizes
     s, t, b = lax.axis_index("seq"), lax.axis_index("tensor"), lax.axis_index("bucket")
@@ -180,14 +180,10 @@
 
             spread(t + k)
 
-    start_qkv(0)
     weight[
         pl.ds(pl.multiple_of(b * w_rows, w_rows), w_rows),
         pl.ds(pl.multiple_of(t * w_cols, w_cols), w_cols),
     ] = w_ref[...]
-    spread(t)
-    for h in range(1, heads):
-        start_qkv(h)
 
     @pl.when(t < n_tensor - 1)
     def _():
@@ -196,6 +192,9 @@
     @pl.when(t > 0)
     def _():
         down_copy(t).start()
+
+    start_qkv(0)
+    spread(t)
 
     for h in range(heads):
         cols = pl.ds(pl.multiple_of((me * heads + h) * HS, HS), HS)
@@ -206,18 +205,23 @@
     index = lax.broadcasted_iota(jnp.int32, (1, total), 1)
     token = (index % block // rows * n_tensor + index // block) * rows + index % rows
     usable = token < live
-    row_index = lax.broadcasted_iota(jnp.int32, (block, 1), 0)
     factor = HS ** (-0.5) * math.log2(math.e)
 
-    def att_copy(h, step, target, source):
-        here = pl.ds(pl.multiple_of(target * block, block), block)
+    def slot_of(side):
+        return (side + s) % 2
+
+    def att_copy(h, step, target, source, side=None):
+        first, count, slot = (0, block, 0) if side is None else (side * rows, rows, slot_of(side))
+        here = pl.ds(pl.multiple_of(target * block + first, rows), count)
+        there = pl.ds(pl.multiple_of(first, rows), count)
         cols = pl.ds(pl.multiple_of((source * heads + h) * HS, HS), HS)
         return remote(
-            done.at[h, here, :], mixed.at[:, cols], att_send.at[h, step], att_recv.at[h, step], device(s, target, b)
-        )
-
-    def attend(h, target):
-        here = pl.ds(pl.multiple_of(target * block, block), block)
+            done.at[h, here, :], mixed.at[there, cols],
+            att_send.at[h, slot, step], att_recv.at[h, slot, step], device(s, target, b),
+        )
+
+    def attend(h, target, first, count):
+        here = pl.ds(pl.multiple_of(target * block + first, rows), count)
         scores = lax.dot_general(
             got[h, 0, here, :], got[h, 1], (((1,), (1,)), ((), ())), preferred_element_type=jnp.float32
         )
@@ -226,10 +230,30 @@
         expo = jnp.exp2((scores - peak) * factor)
         denominator = jnp.sum(expo, axis=-1, keepdims=True)
         result = jnp.dot(expo.astype(jnp.bfloat16), got[h, 2], preferred_element_type=jnp.float32) / denominator
-        own_token = (row_index // rows * n_tensor + target) * rows + row_index % rows
+        row = first + lax.broadcasted_iota(jnp.int32, (count, 1), 0)
+        own_token = (row // rows * n_tensor + target) * rows + row % rows
         return jnp.where(own_token < live, result, 0.0).astype(jnp.bfloat16)
 
+    def attend_all(h, first, count, side):
+        def one(step, carry):
+            target = (t + step) % n_tensor
+            done[h, pl.ds(pl.multiple_of(target * block + first, rows), count), :] = attend(h, target, first, count)
+            att_copy(h, step, target, t, side).start()
+            return carry
+
+        lax.fori_loop(1, n_tensor, one, 0)
+        mixed[
+            pl.ds(pl.multiple_of(first, rows), count), pl.ds(pl.multiple_of((t * heads + h) * HS, HS), HS)
+        ] = attend(h, t, first, count)
+
+    relayed = 1
     for h in range(heads):
+        if relayed < n_tensor:
+            relay(relayed)
+            relayed += 1
+        if h + 1 < heads:
+            start_qkv(h + 1)
+
         def arrive(step, carry):
             source = (me + group - step) % group
             for j in range(3):
@@ -237,19 +261,12 @@
             return carry
 
         lax.fori_loop(1, group, arrive, 0)
-
-        def one(step, carry):
-            target = (t + step) % n_tensor
-            here = pl.ds(pl.multiple_of(target * block, block), block)
-            done[h, here, :] = attend(h, target)
-            att_copy(h, step, target, t).start()
-            return carry
-
-        lax.fori_loop(1, n_tensor, one, 0)
-        mixed[:, pl.ds(pl.multiple_of((t * heads + h) * HS, HS), HS)] = attend(h, t)
-        if h + 1 < n_tensor:
-            relay(h + 1)
-    for k in range(heads + 1, n_tensor):
+        if h + 1 < heads:
+            attend_all(h, 0, block, None)
+        else:
+            attend_all(h, (1 - s) * rows, rows, 1 - s)
+            attend_all(h, s * rows, rows, s)
+    for k in range(relayed, n_tensor):
         relay(k)
 
     for p in range(n_tensor):
@@ -258,12 +275,12 @@
     for p in range(n_tensor):
         near_copy(0, p, near).wait_recv()
         near_copy(1, p, (near + 2) % 4).wait_recv()
-    for h in range(heads):
-        def back(step, carry):
-            att_copy(h, step, t, (t + n_tensor - step) % n_tensor).wait_recv()
-            return carry
-
-        lax.fori_loop(1, n_tensor, back, 0)
+    def back(h, side):
+        def body(step, carry):
+            att_copy(h, step, t, (t + n_tensor - step) % n_tensor, side).wait_recv()
+            return carry
+
+        lax.fori_loop(1, n_tensor, body, 0)
 
     def part_copy(p):
         cut = slice(p * w_cols, (p + 1) * w_cols)
@@ -271,17 +288,32 @@
             part_out.at[:, cut], part_in.at[:, cut], part_send.at[p], part_recv.at[p], device(1 - s, t, b)
         )
 
-    for p in range(n_tensor):
+    def leave(p):
         cut = slice(p * w_cols, (p + 1) * w_cols)
-        summed = jnp.dot(mixed[...], weight[:, cut], preferred_element_type=jnp.float32)
-        first, second = summed[:rows], summed[rows:]
-        part_out[:, cut] = jnp.where(s == 0, second, first).astype(jnp.bfloat16)
+        return pltpu.make_async_copy(part_in.at[:, cut], out_ref.at[0, :, cut], out_sem.at[p])
+
+    for h in range(heads - 1):
+        back(h, None)
+    back(heads - 1, 1 - s)
+    for p in range(n_tensor):
+        cut = slice(p * w_cols, (p + 1) * w_cols)
+        part_out[:, cut] = jnp.dot(
+            mixed[pl.ds(pl.multiple_of((1 - s) * rows, rows), rows), :], weight[:, cut],
+            preferred_element_type=jnp.float32,
+        ).astype(jnp.bfloat16)
         part_copy(p).start()
-        own_part[:, cut] = jnp.where(s == 0, first, second)
+    back(heads - 1, s)
+    for p in range(n_tensor):
+        cut = slice(p * w_cols, (p + 1) * w_cols)
+        own_part[:, cut] = jnp.dot(
+            mixed[pl.ds(pl.multiple_of(s * rows, rows), rows), :], weight[:, cut],
+            preferred_element_type=jnp.float32,
+        )
     for p in range(n_tensor):
         cut = slice(p * w_cols, (p + 1) * w_cols)
         part_copy(p).wait_recv()
-        out_ref[0, :, cut] = (own_part[:, cut] + part_in[:, cut].astype(jnp.float32)).astype(jnp.bfloat16)
+        part_in[:, cut] = (own_part[:, cut] + part_in[:, cut].astype(jnp.float32)).astype(jnp.bfloat16)
+        leave(p).start()
 
     for h in range(heads):
         def sent(step, carry):
@@ -293,7 +325,11 @@
         lax.fori_loop(1, group, sent, 0)
 
         def att_sent(step, carry):
-            att_copy(h, step, (t + step) % n_tensor, t).wait_send()
+            if h + 1 < heads:
+                att_copy(h, step, (t + step) % n_tensor, t).wait_send()
+            else:
+                att_copy(h, step, (t + step) % n_tensor, t, 1 - s).wait_send()
+                att_copy(h, step, (t + step) % n_tensor, t, s).wait_send()
             return carry
 
         lax.fori_loop(1, n_tensor, att_sent, 0)
@@ -311,6 +347,7 @@
         near_copy(0, p, b).wait_send()
         near_copy(1, p, far).wait_send()
         part_copy(p).wait_send()
+        leave(p).wait()
 
 
 def fused(axes, sizes, queries, keys, values, lengths, out_weight):
@@ -326,7 +363,7 @@
         functools.partial(whole_kernel, axes, sizes),
         out_shape=jax.ShapeDtypeStruct(queries.shape, queries.dtype),
         in_specs=[pl.BlockSpec(memory_space=pltpu.SMEM), vmem, vmem, vmem, vmem],
-        out_specs=vmem,
+        out_specs=pl.BlockSpec(memory_space=pl.ANY),
         scratch_shapes=[
             pltpu.VMEM((heads, 3, total, HS), jnp.bfloat16),
             pltpu.VMEM((heads, total, HS), jnp.bfloat16),
@@ -337,8 +374,8 @@
             pltpu.VMEM((rows, width), jnp.float32),
             dma((heads, 3, group)),
             dma((heads, 3, group)),
-            dma((heads, n_tensor)),
-            dma((heads, n_tensor)),
+            dma((heads, 2, n_tensor)),
+            dma((heads, 2, n_tensor)),
             dma((n_tensor,)),
             dma((n_tensor,)),
             dma((n_tensor,)),
@@ -346,6 +383,7 @@
             dma((n_tensor,)),
             dma((2, n_tensor)),
             dma((2, n_tensor)),
+            dma((n_tensor,)),
             dma((n_tensor,)),
             dma((n_tensor,)),
         ],

time: 155 us -> 140 us (0.903)
  Pallas kernels: 151 us -> 136 us
    pallas_call x1, Pallas kernels: 151 us -> 136 us  [fused(): pl.pallas_call(functools.partial(whole_kernel, axes, sizes), out_shape=ja...]
where the time goes in v2:
time: 140 us; the launch traced here: 139 us
  Pallas kernels  136 us (97%)
  local copies, waits for them, and re-layouts  2.06 us (1%)
    pallas_call x1, Pallas kernels, fused(): pl.pallas_call(functools.partial(whole_kernel, axes, sizes), out_shape=ja...  136 us

profile of v2, /device:TPU:0, one launch (start us, length us, event | category | flops | bytes accessed | tf_op | source)
XLA Modules:
  0.0 139.2 jit_solution(17847802325369019063)
XLA Ops:
  0.7 136.5 %shard_map.55 = bf16[1,128,3072]{2,1,0:T(8,128)(2,1)} custom-call(s32[1]{0:T(128)S(6)} %copy.7.len_ref, bf16[1,128,3072]{2,1,0:T(8,128)(2,1)} %q_ref.1, bf16[1,128,3072]{2,1,0:T(8,128)(2,1)} %k_ref.1, bf16[1,128,3072]{2,1,0:T(8,128)(2,1)} %v_ref.1, bf16[384,768]{1,0:T(8,128)(2,1)} %w_ref.1), custom_call_target="tpu_custom_call" | custom-call | tf_op jit(solution)/shard_map/pallas_call | solution.py:362
  137.1 2.1 %copy.8 = bf16[1,128,3072]{2,1,0:T(8,128)(2,1)} copy(bf16[1,128,3072]{2,1,0:T(8,128)(2,1)} %shard_map.55) | data formatting | bytes 1572864

commit v3 on v2

--- a/solution.py
+++ b/solution.py
@@ -246,13 +246,20 @@
             pl.ds(pl.multiple_of(first, rows), count), pl.ds(pl.multiple_of((t * heads + h) * HS, HS), HS)
         ] = attend(h, t, first, count)
 
-    relayed = 1
+    upper = t // 2
+    order = (t, 1 - t + 4 * upper, 2 - upper, 3 - 3 * upper)
+
+    def forward(p):
+        far_copy(p, far).wait_recv()
+        near_copy(1, p, far).start()
+
     for h in range(heads):
-        if relayed < n_tensor:
-            relay(relayed)
-            relayed += 1
-        if h + 1 < heads:
-            start_qkv(h + 1)
+        if h == 0:
+            relay(1)
+            for later in range(1, heads):
+                start_qkv(later)
+        elif h == 1:
+            relay(2)
 
         def arrive(step, carry):
             source = (me + group - step) % group
@@ -261,20 +268,18 @@
             return carry
 
         lax.fori_loop(1, group, arrive, 0)
+        if 1 <= h <= 2:
+            forward(order[h - 1])
         if h + 1 < heads:
             attend_all(h, 0, block, None)
         else:
             attend_all(h, (1 - s) * rows, rows, 1 - s)
             attend_all(h, s * rows, rows, s)
-    for k in range(relayed, n_tensor):
+    for k in range(heads, 3):
         relay(k)
-
-    for p in range(n_tensor):
-        far_copy(p, far).wait_recv()
-        near_copy(1, p, far).start()
-    for p in range(n_tensor):
-        near_copy(0, p, near).wait_recv()
-        near_copy(1, p, (near + 2) % 4).wait_recv()
+    for k in range(max(heads - 1, 0), 3):
+        forward(order[k])
+
     def back(h, side):
         def body(step, carry):
             att_copy(h, step, t, (t + n_tensor - step) % n_tensor, side).wait_recv()
@@ -282,35 +287,44 @@
 
         lax.fori_loop(1, n_tensor, body, 0)
 
+    def cut_of(p):
+        return pl.ds(pl.multiple_of(p * w_cols, w_cols), w_cols)
+
     def part_copy(p):
-        cut = slice(p * w_cols, (p + 1) * w_cols)
+        cut = cut_of(p)
         return remote(
             part_out.at[:, cut], part_in.at[:, cut], part_send.at[p], part_recv.at[p], device(1 - s, t, b)
         )
 
     def leave(p):
-        cut = slice(p * w_cols, (p + 1) * w_cols)
+        cut = cut_of(p)
         return pltpu.make_async_copy(part_in.at[:, cut], out_ref.at[0, :, cut], out_sem.at[p])
 
     for h in range(heads - 1):
         back(h, None)
     back(heads - 1, 1 - s)
-    for p in range(n_tensor):
-        cut = slice(p * w_cols, (p + 1) * w_cols)
+    for k, p in enumerate(order):
+        near_copy(0, p, near).wait_recv()
+        near_copy(1, p, (near + 2) % 4).wait_recv()
+        cut = cut_of(p)
         part_out[:, cut] = jnp.dot(
             mixed[pl.ds(pl.multiple_of((1 - s) * rows, rows), rows), :], weight[:, cut],
             preferred_element_type=jnp.float32,
         ).astype(jnp.bfloat16)
         part_copy(p).start()
+        if k == 0:
+            relay(3)
+        if k == 2:
+            forward(order[3])
     back(heads - 1, s)
-    for p in range(n_tensor):
-        cut = slice(p * w_cols, (p + 1) * w_cols)
+    for p in order:
+        cut = cut_of(p)
         own_part[:, cut] = jnp.dot(
             mixed[pl.ds(pl.multiple_of(s * rows, rows), rows), :], weight[:, cut],
             preferred_element_type=jnp.float32,
         )
-    for p in range(n_tensor):
-        cut = slice(p * w_cols, (p + 1) * w_cols)
+    for p in order:
+        cut = cut_of(p)
         part_copy(p).wait_recv()
         part_in[:, cut] = (own_part[:, cut] + part_in[:, cut].astype(jnp.float32)).astype(jnp.bfloat16)
         leave(p).start()

time: 140 us -> 132 us (0.943)
  Pallas kernels: 136 us -> 128 us
    pallas_call x1, Pallas kernels: 136 us -> 128 us  [fused(): pl.pallas_call(functools.partial(whole_kernel, axes, sizes), out_shape=ja...]
where the time goes in v3:
time: 132 us; the launch traced here: 131 us
  Pallas kernels  128 us (97%)
  local copies, waits for them, and re-layouts  2.06 us (2%)
    pallas_call x1, Pallas kernels, fused(): pl.pallas_call(functools.partial(whole_kernel, axes, sizes), out_shape=ja...  128 us

profile of v3, /device:TPU:0, one launch (start us, length us, event | category | flops | bytes accessed | tf_op | source)
XLA Modules:
  0.0 131.0 jit_solution(14439357890260157270)
XLA Ops:
  0.7 128.3 %shard_map.55 = bf16[1,128,3072]{2,1,0:T(8,128)(2,1)} custom-call(s32[1]{0:T(128)S(6)} %copy.7.len_ref, bf16[1,128,3072]{2,1,0:T(8,128)(2,1)} %q_ref.1, bf16[1,128,3072]{2,1,0:T(8,128)(2,1)} %k_ref.1, bf16[1,128,3072]{2,1,0:T(8,128)(2,1)} %v_ref.1, bf16[384,768]{1,0:T(8,128)(2,1)} %w_ref.1), custom_call_target="tpu_custom_call" | custom-call | tf_op jit(solution)/shard_map/pallas_call | solution.py:376
  128.9 2.1 %copy.8 = bf16[1,128,3072]{2,1,0:T(8,128)(2,1)} copy(bf16[1,128,3072]{2,1,0:T(8,128)(2,1)} %shard_map.55) | data formatting | bytes 1572864

commit v4 on v3

--- a/solution.py
+++ b/solution.py
@@ -222,16 +222,18 @@
 
     def attend(h, target, first, count):
         here = pl.ds(pl.multiple_of(target * block + first, rows), count)
+        row = first + lax.broadcasted_iota(jnp.int32, (count, 1), 0)
+        return attend_rows(h, got[h, 0, here, :], (row // rows * n_tensor + target) * rows + row % rows)
+
+    def attend_rows(h, query, own_token):
         scores = lax.dot_general(
-            got[h, 0, here, :], got[h, 1], (((1,), (1,)), ((), ())), preferred_element_type=jnp.float32
+            query, got[h, 1], (((1,), (1,)), ((), ())), preferred_element_type=jnp.float32
         )
         scores = jnp.where(usable, scores, MASKED_SCORE)
         peak = jnp.max(scores, axis=-1, keepdims=True)
         expo = jnp.exp2((scores - peak) * factor)
         denominator = jnp.sum(expo, axis=-1, keepdims=True)
         result = jnp.dot(expo.astype(jnp.bfloat16), got[h, 2], preferred_element_type=jnp.float32) / denominator
-        row = first + lax.broadcasted_iota(jnp.int32, (count, 1), 0)
-        own_token = (row // rows * n_tensor + target) * rows + row % rows
         return jnp.where(own_token < live, result, 0.0).astype(jnp.bfloat16)
 
     def attend_all(h, first, count, side):
@@ -245,6 +247,26 @@
         mixed[
             pl.ds(pl.multiple_of(first, rows), count), pl.ds(pl.multiple_of((t * heads + h) * HS, HS), HS)
         ] = attend(h, t, first, count)
+
+    def attend_side(h, side):
+        row = lax.broadcasted_iota(jnp.int32, (rows, 1), 0)
+        for step in range(0, n_tensor, 2):
+            targets = [(t + step + i) % n_tensor for i in (1, 2)]
+            spans = [pl.ds(pl.multiple_of(target * block + side * rows, rows), rows) for target in targets]
+            result = attend_rows(
+                h,
+                jnp.concatenate([got[h, 0, span, :] for span in spans], axis=0),
+                jnp.concatenate([(side * n_tensor + target) * rows + row for target in targets], axis=0),
+            )
+            for i in range(2):
+                if step + i + 1 < n_tensor:
+                    done[h, spans[i], :] = result[i * rows : (i + 1) * rows]
+                    att_copy(h, step + i + 1, targets[i], t, side).start()
+                else:
+                    mixed[
+                        pl.ds(pl.multiple_of(side * rows, rows), rows),
+                        pl.ds(pl.multiple_of((t * heads + h) * HS, HS), HS),
+                    ] = result[i * rows : (i + 1) * rows]
 
     upper = t // 2
     order = (t, 1 - t + 4 * upper, 2 - upper, 3 - 3 * upper)
@@ -273,8 +295,8 @@
         if h + 1 < heads:
             attend_all(h, 0, block, None)
         else:
-            attend_all(h, (1 - s) * rows, rows, 1 - s)
-            attend_all(h, s * rows, rows, s)
+            attend_side(h, 1 - s)
+            attend_side(h, s)
     for k in range(heads, 3):
         relay(k)
     for k in range(max(heads - 1, 0), 3):

time: 132 us -> 132 us (level)
  no operation moved by 1% of the time
where the time goes in v4:
time: 132 us; the launch traced here: 131 us
  Pallas kernels  128 us (97%)
  local copies, waits for them, and re-layouts  2.06 us (2%)
    pallas_call x1, Pallas kernels, fused(): pl.pallas_call(functools.partial(whole_kernel, axes, sizes), out_shape=ja...  128 us

profile of v4, /device:TPU:0, one launch (start us, length us, event | category | flops | bytes accessed | tf_op | source)
XLA Modules:
  0.0 131.0 jit_solution(6324172747448554304)
XLA Ops:
  0.7 128.3 %shard_map.55 = bf16[1,128,3072]{2,1,0:T(8,128)(2,1)} custom-call(s32[1]{0:T(128)S(6)} %copy.7.len_ref, bf16[1,128,3072]{2,1,0:T(8,128)(2,1)} %q_ref.1, bf16[1,128,3072]{2,1,0:T(8,128)(2,1)} %k_ref.1, bf16[1,128,3072]{2,1,0:T(8,128)(2,1)} %v_ref.1, bf16[384,768]{1,0:T(8,128)(2,1)} %w_ref.1), custom_call_target="tpu_custom_call" | custom-call | tf_op jit(solution)/shard_map/pallas_call | solution.py:398
  128.9 2.1 %copy.8 = bf16[1,128,3072]{2,1,0:T(8,128)(2,1)} copy(bf16[1,128,3072]{2,1,0:T(8,128)(2,1)} %shard_map.55) | data formatting | bytes 1572864

commit v5 on v3

--- a/solution.py
+++ b/solution.py
@@ -256,10 +256,13 @@
     for h in range(heads):
         if h == 0:
             relay(1)
-            for later in range(1, heads):
-                start_qkv(later)
+            start_qkv(1)
         elif h == 1:
             relay(2)
+            for later in range(2, heads):
+                start_qkv(later)
+        elif h == 2:
+            relay(3)
 
         def arrive(step, carry):
             source = (me + group - step) % group
@@ -312,8 +315,6 @@
             preferred_element_type=jnp.float32,
         ).astype(jnp.bfloat16)
         part_copy(p).start()
-        if k == 0:
-            relay(3)
         if k == 2:
             forward(order[3])
     back(heads - 1, s)

time: 132 us -> 135 us (1.023)
  Pallas kernels: 128 us -> 132 us
    pallas_call x1, Pallas kernels: 128 us -> 132 us  [fused(): pl.pallas_call(functools.partial(whole_kernel, axes, sizes), out_shape=ja...]
where the time goes in v5:
time: 135 us
  Pallas kernels  132 us (98%)
  local copies, waits for them, and re-layouts  2.06 us (2%)
    pallas_call x1, Pallas kernels, fused(): pl.pallas_call(functools.partial(whole_kernel, axes, sizes), out_shape=ja...  132 us

profile of v5, /device:TPU:0, one launch (start us, length us, event | category | flops | bytes accessed | tf_op | source)
XLA Modules:
  0.0 134.6 jit_solution(17010718368419019794)
XLA Ops:
  0.7 131.8 %shard_map.55 = bf16[1,128,3072]{2,1,0:T(8,128)(2,1)} custom-call(s32[1]{0:T(128)S(6)} %copy.7.len_ref, bf16[1,128,3072]{2,1,0:T(8,128)(2,1)} %q_ref.1, bf16[1,128,3072]{2,1,0:T(8,128)(2,1)} %k_ref.1, bf16[1,128,3072]{2,1,0:T(8,128)(2,1)} %v_ref.1, bf16[384,768]{1,0:T(8,128)(2,1)} %w_ref.1), custom_call_target="tpu_custom_call" | custom-call | tf_op jit(solution)/shard_map/pallas_call | solution.py:377
  132.5 2.1 %copy.8 = bf16[1,128,3072]{2,1,0:T(8,128)(2,1)} copy(bf16[1,128,3072]{2,1,0:T(8,128)(2,1)} %shard_map.55) | data formatting | bytes 1572864
